TPU v7x, 32 devices: a whole 2x2x4 slice. The times are simulated.
32 devices in a mesh: row: 4 (over x, core), col: 8 (over z, y).
Axes of the slice: x: 2, y: 2, z: 4, core: 2. Of those that a mesh axis runs over, the one named last changes fastest.
Arguments:
- w_rec: bfloat16 [2, 4096, 4, 4096], P(None, 'row', None, 'col'), may hold values from -0.09375 to 0.09375
- w_in: bfloat16 [2, 4096, 4, 4096], P(None, 'row', None, 'col'), may hold values from -0.09375 to 0.09375
- gate_pre: float32 [2, 6, 64, 4, 4096], P(None, None, None, None, 'col'), may hold values from -8 to 8, as said below
- cells: float32 [2, 7, 64, 4096], P(None, None, None, 'col'), may hold values from -6 to 6
- layer_in: bfloat16 [2, 6, 64, 4096], P(None, None, None, 'row'), may hold values from -1 to 1
- h_prev: bfloat16 [2, 6, 64, 4096], P(None, None, None, 'row'), may hold values from -1 to 1
- top_grad: float32 [6, 64, 4096], P(None, None, 'col'), may hold values from -40 to 40
Outputs:
- w_rec_grad: bfloat16 [2, 4096, 4, 4096], P(None, 'row', None, 'col')
- w_in_grad: bfloat16 [2, 4096, 4, 4096], P(None, 'row', None, 'col')
- input_grad: float32 [6, 64, 4096], P(None, None, 'col')
Inputs may be any that keep to these rules, and one draw needn't show every extreme that they name: `gate_pre`: dimension 3 holds the input, forget, candidate and output gates in that order.
All inputs are finite; a program needn't handle non-finite values.
Results may differ from a plain program's by a relative error of at most 0.0051.
Values sent between devices are 32-bit elements; how exact they have to be, the bound alone decides.
A program may use at most 128 MiB of HBM per device.

v0:
```python
import jax
import jax.numpy as jnp
from jax import lax
from jax.sharding import PartitionSpec as P

WIDTH = 4096
LAYERS = 2


def from_root(block, axis, owner):
    block = jnp.where(lax.axis_index(axis) == owner, block, jnp.zeros_like(block))
    return lax.psum(block, axis)


def cell_backward(preact, cell_prev, cell_now, hid_grad, cell_carry):
    in_gate = jax.nn.sigmoid(preact[:, 0])
    forget = jax.nn.sigmoid(preact[:, 1])
    cand_gate = jnp.tanh(preact[:, 2])
    out_gate = jax.nn.sigmoid(preact[:, 3])
    tanh_cell = jnp.tanh(cell_now)
    cell_grad = cell_carry + hid_grad * out_gate * (1.0 - tanh_cell * tanh_cell)
    grad_in = cell_grad * cand_gate * in_gate * (1.0 - in_gate)
    grad_forget = cell_grad * cell_prev * forget * (1.0 - forget)
    grad_cand = cell_grad * in_gate * (1.0 - cand_gate * cand_gate)
    grad_out = hid_grad * tanh_cell * out_gate * (1.0 - out_gate)
    gate_grads = jnp.stack([grad_in, grad_forget, grad_cand, grad_out], axis=1).astype(jnp.bfloat16)
    return (gate_grads, cell_grad * forget)


def contract_gates(gate_flat, weight_flat):
    return lax.dot_general(
        gate_flat, weight_flat, (((1,), (1,)), ((), ())), preferred_element_type=jnp.float32
    )


def own_block(total):
    ratio = lax.axis_size("col") // lax.axis_size("row")
    width = total.shape[-1] // ratio
    column = lax.axis_index("col")
    piece = lax.dynamic_slice_in_dim(total, column % ratio * width, width, total.ndim - 1)
    return (piece, column // ratio)


def wave_units(partial_value):
    piece, root = own_block(lax.psum(partial_value, "col"))
    return from_root(piece, "row", root)


def input_units(partial_value):
    piece, root = own_block(lax.psum(partial_value, "col"))
    return from_root(piece, "row", root)


def local(w_rec, w_in, gate_pre, cells, layer_in, h_prev, top_grad):
    layers = w_rec.shape[0]
    row_units = w_rec.shape[1]
    steps, batch, col_units = top_grad.shape
    rec_flats = [w_rec[layer].reshape(row_units, 4 * col_units) for layer in range(layers)]
    in_flats = [w_in[layer].reshape(row_units, 4 * col_units) for layer in range(layers)]
    gate_store = [None] * layers
    zeros = jnp.zeros((layers, batch, col_units), jnp.float32)
    empty = tuple(
        (jnp.zeros((steps, batch, 4, col_units), jnp.bfloat16) for layer in range(layers))
    )

    def diagonal_step(diagonal, carry):
        rec_carry, cell_carry, above, stores = carry
        partials = []
        dx_partials = []
        new_cells = []
        new_stores = []
        for layer in range(layers):
            depth = layers - 1 - layer
            step_idx = steps - 1 - diagonal + depth
            valid = (step_idx >= 0) & (step_idx < steps)
            clamped = jnp.clip(step_idx, 0, steps - 1).astype(jnp.int32)
            preact = lax.dynamic_index_in_dim(gate_pre[layer], clamped, 0, keepdims=False)
            cell_prev = lax.dynamic_index_in_dim(cells[layer], clamped, 0, keepdims=False)
            cell_now = lax.dynamic_index_in_dim(cells[layer], clamped + 1, 0, keepdims=False)
            if layer == layers - 1:
                outside = lax.dynamic_index_in_dim(top_grad, clamped, 0, keepdims=False)
            else:
                outside = above[layer]
            gate_grads, cell_next = cell_backward(
                preact, cell_prev, cell_now, outside + rec_carry[layer], cell_carry[layer]
            )
            gate_grads = jnp.where(valid, gate_grads, jnp.zeros_like(gate_grads))
            cell_next = jnp.where(valid, cell_next, jnp.zeros_like(cell_next))
            previous = lax.dynamic_index_in_dim(stores[layer], clamped, 0, keepdims=False)
            written = jnp.where(valid, gate_grads, previous)
            new_stores.append(lax.dynamic_update_index_in_dim(stores[layer], written, clamped, 0))
            gate_flat = gate_grads.reshape(batch, 4 * col_units)
            partials.append(contract_gates(gate_flat, rec_flats[layer]))
            if layer > 0:
                dx_partials.append(contract_gates(gate_flat, in_flats[layer]))
            new_cells.append(cell_next)
        units = wave_units(jnp.concatenate(partials + dx_partials, axis=0))
        rec_next = jnp.stack(
            [units[layer * batch : (layer + 1) * batch] for layer in range(layers)]
        )
        above_list = [units[layers * batch : (layers + 1) * batch]]
        above_next = jnp.stack(above_list + [jnp.zeros((batch, col_units), jnp.float32)])
        return (rec_next, jnp.stack(new_cells), above_next, tuple(new_stores))

    final = lax.fori_loop(0, steps + layers - 1, diagonal_step, (zeros, zeros, zeros, empty))
    for layer in range(layers):
        gate_store[layer] = final[3][layer].reshape(steps * batch, 4 * col_units)
    input_grad = input_units(contract_gates(gate_store[0], in_flats[0])).reshape(
        steps, batch, col_units
    )
    rec_grads = []
    in_grads = []
    partial_sums = []
    for layer in range(layers):
        raw_rec = lax.dot_general(
            h_prev[layer].reshape(steps * batch, row_units),
            gate_store[layer],
            (((0,), (0,)), ((), ())),
            preferred_element_type=jnp.float32,
        )
        raw_in = lax.dot_general(
            layer_in[layer].reshape(steps * batch, row_units),
            gate_store[layer],
            (((0,), (0,)), ((), ())),
            preferred_element_type=jnp.float32,
        )
        rec_grads.append(raw_rec)
        in_grads.append(raw_in)
        partial_sums.append(jnp.sum(raw_rec * raw_rec) + jnp.sum(raw_in * raw_in))
    totals = [lax.psum(partial_value, ("row", "col")) for partial_value in partial_sums]
    sumsq = totals[0]
    for extra in totals[1:]:
        sumsq = sumsq + extra
    scale = 1.0 / jnp.maximum(jnp.sqrt(sumsq / (8.0 * LAYERS * WIDTH * WIDTH)), 0.05)
    w_rec_grad = jnp.stack(
        [(rec_grads[layer] * scale).reshape(row_units, 4, col_units) for layer in range(layers)]
    ).astype(jnp.bfloat16)
    w_in_grad = jnp.stack(
        [(in_grads[layer] * scale).reshape(row_units, 4, col_units) for layer in range(layers)]
    ).astype(jnp.bfloat16)
    return (w_rec_grad, w_in_grad, input_grad)


def solution(mesh):
    placed = (
        P(None, "row", None, "col"),
        P(None, "row", None, "col"),
        P(None, None, None, None, "col"),
        P(None, None, None, "col"),
        P(None, None, None, "row"),
        P(None, None, None, "row"),
        P(None, None, "col"),
    )
    return jax.shard_map(
        local,
        mesh=mesh,
        in_specs=placed,
        out_specs=(P(None, "row", None, "col"), P(None, "row", None, "col"), P(None, None, "col")),
        check_vma=False,
    )
```

profile of v0, /device:TPU:0, one launch (start us, length us, event | category | flops | bytes accessed | tf_op | source)
XLA Modules:
  0.0 1127.2 jit_solution(5628223669936796487)
XLA Ops:
  43.4 897.5 %while.24 = (s32[]{:T(128)}, f32[2,64,512]{2,1,0:T(8,128)S(1)}, f32[2,64,512]{2,1,0:T(8,128)S(1)}, f32[2,64,512]{2,1,0:T(8,128)}, bf16[6,64,4,512]{3,2,1,0:T(4,1...) while((s32[]{:T(128)}, f32[2,64,512]{2,1,0:T(8,128)S(1)}, ...), condition=%wide.region_3.4_spmd, body=%wide.region_0.3_spmd.sunk | while | flops 811958272 | bytes 109184224 | solution.py:105
  73.1 75.5 %all-reduce.10.cloned.1.call-done = f32[192,1024]{1,0:T(8,128)} async-done(((f32[192,1024]{1,0:T(8,128)}), f32[192,1024]{1,0:T(8,128)}) %all-reduce.10.cloned.1.call-update) | async-done | bytes 786448 | tf_op jit(solution)/shard_map/while/body/eval_jaxpr/psum | solution.py:45
  151.6 31.3 %all-reduce.12.cloned.1.call-done = f32[192,512]{1,0:T(8,128)} async-done(((f32[192,512]{1,0:T(8,128)}), f32[192,512]{1,0:T(8,128)}) %all-reduce.12.cloned.1.call-update) | async-done | bytes 393232 | tf_op jit(solution)/shard_map/while/body/eval_jaxpr/psum | solution.py:12
  201.9 72.8 %all-reduce.10.cloned.1.call-done = f32[192,1024]{1,0:T(8,128)} async-done(((f32[192,1024]{1,0:T(8,128)}), f32[192,1024]{1,0:T(8,128)}) %all-reduce.10.cloned.1.call-update) | async-done | bytes 786448 | tf_op jit(solution)/shard_map/while/body/eval_jaxpr/psum | solution.py:45
  277.7 31.2 %all-reduce.12.cloned.1.call-done = f32[192,512]{1,0:T(8,128)} async-done(((f32[192,512]{1,0:T(8,128)}), f32[192,512]{1,0:T(8,128)}) %all-reduce.12.cloned.1.call-update) | async-done | bytes 393232 | tf_op jit(solution)/shard_map/while/body/eval_jaxpr/psum | solution.py:12
  327.9 72.8 %all-reduce.10.cloned.1.call-done = f32[192,1024]{1,0:T(8,128)} async-done(((f32[192,1024]{1,0:T(8,128)}), f32[192,1024]{1,0:T(8,128)}) %all-reduce.10.cloned.1.call-update) | async-done | bytes 786448 | tf_op jit(solution)/shard_map/while/body/eval_jaxpr/psum | solution.py:45
  403.7 31.2 %all-reduce.12.cloned.1.call-done = f32[192,512]{1,0:T(8,128)} async-done(((f32[192,512]{1,0:T(8,128)}), f32[192,512]{1,0:T(8,128)}) %all-reduce.12.cloned.1.call-update) | async-done | bytes 393232 | tf_op jit(solution)/shard_map/while/body/eval_jaxpr/psum | solution.py:12
  453.9 72.8 %all-reduce.10.cloned.1.call-done = f32[192,1024]{1,0:T(8,128)} async-done(((f32[192,1024]{1,0:T(8,128)}), f32[192,1024]{1,0:T(8,128)}) %all-reduce.10.cloned.1.call-update) | async-done | bytes 786448 | tf_op jit(solution)/shard_map/while/body/eval_jaxpr/psum | solution.py:45
  529.7 31.3 %all-reduce.12.cloned.1.call-done = f32[192,512]{1,0:T(8,128)} async-done(((f32[192,512]{1,0:T(8,128)}), f32[192,512]{1,0:T(8,128)}) %all-reduce.12.cloned.1.call-update) | async-done | bytes 393232 | tf_op jit(solution)/shard_map/while/body/eval_jaxpr/psum | solution.py:12
  580.1 72.8 %all-reduce.10.cloned.1.call-done = f32[192,1024]{1,0:T(8,128)} async-done(((f32[192,1024]{1,0:T(8,128)}), f32[192,1024]{1,0:T(8,128)}) %all-reduce.10.cloned.1.call-update) | async-done | bytes 786448 | tf_op jit(solution)/shard_map/while/body/eval_jaxpr/psum | solution.py:45
  655.9 31.1 %all-reduce.12.cloned.1.call-done = f32[192,512]{1,0:T(8,128)} async-done(((f32[192,512]{1,0:T(8,128)}), f32[192,512]{1,0:T(8,128)}) %all-reduce.12.cloned.1.call-update) | async-done | bytes 393232 | tf_op jit(solution)/shard_map/while/body/eval_jaxpr/psum | solution.py:12
  706.1 72.8 %all-reduce.10.cloned.1.call-done = f32[192,1024]{1,0:T(8,128)} async-done(((f32[192,1024]{1,0:T(8,128)}), f32[192,1024]{1,0:T(8,128)}) %all-reduce.10.cloned.1.call-update) | async-done | bytes 786448 | tf_op jit(solution)/shard_map/while/body/eval_jaxpr/psum | solution.py:45
  781.9 31.1 %all-reduce.12.cloned.1.call-done = f32[192,512]{1,0:T(8,128)} async-done(((f32[192,512]{1,0:T(8,128)}), f32[192,512]{1,0:T(8,128)}) %all-reduce.12.cloned.1.call-update) | async-done | bytes 393232 | tf_op jit(solution)/shard_map/while/body/eval_jaxpr/psum | solution.py:12
  832.1 72.8 %all-reduce.10.cloned.1.call-done = f32[192,1024]{1,0:T(8,128)} async-done(((f32[192,1024]{1,0:T(8,128)}), f32[192,1024]{1,0:T(8,128)}) %all-reduce.10.cloned.1.call-update) | async-done | bytes 786448 | tf_op jit(solution)/shard_map/while/body/eval_jaxpr/psum | solution.py:45
  907.9 31.1 %all-reduce.12.cloned.1.call-done = f32[192,512]{1,0:T(8,128)} async-done(((f32[192,512]{1,0:T(8,128)}), f32[192,512]{1,0:T(8,128)}) %all-reduce.12.cloned.1.call-update) | async-done | bytes 393232 | tf_op jit(solution)/shard_map/while/body/eval_jaxpr/psum | solution.py:12
  974.7 40.9 %psum.62 = f32[]{:T(128)} all-reduce(f32[]{:T(128)S(6)} %add.481), channel_id=1, replica_groups=mesh['row'=4,'col'=8] {'row','col'}, use_global_device_ids=true, to_apply=%region_6.7 | all-reduce | flops 1 | bytes 8 | tf_op jit(solution)/shard_map/psum | solution.py:130
  1016.4 11.7 %multiply_convert_fusion.4 = (bf16[2048,1024]{1,0:T(8,128)(2,1)}, bf16[2048,1024]{1,0:T(8,128)(2,1)}) fusion(f32[2048,1024]{1,0:T(8,128)} %get-tuple-element.427, f32[]{:T(128)S(6)} %div.192, f32[2048,1024]{1,0:T(8,128)} %get-tuple-element.423), kind=kLoop, calls=%fused_computation.93 | loop fusion | flops 8388608 | bytes 25165828 | tf_op jit(solution)/shard_map/convert.27
  1028.1 11.6 %multiply_convert_fusion.6 = (bf16[2048,1024]{1,0:T(8,128)(2,1)}, bf16[2048,1024]{1,0:T(8,128)(2,1)}) fusion(f32[2048,1024]{1,0:T(8,128)} %get-tuple-element.425, f32[]{:T(128)S(6)} %div.192, f32[2048,1024]{1,0:T(8,128)} %get-tuple-element.421), kind=kLoop, calls=%fused_computation.95 | loop fusion | flops 8388608 | bytes 25165828 | tf_op jit(solution)/shard_map/convert.33
  1039.7 8.0 copy.21
  1047.7 8.0 copy.20
  1063.5 7.9 copy.22
  1071.4 8.7 pad_maximum_fusion.3
  1082.1 8.7 pad_maximum_fusion.4
  1090.8 26.8 %all-reduce.8.cloned.1.call-done = f32[6,64,512]{2,1,0:T(8,128)} async-done(((f32[6,64,512]{2,1,0:T(8,128)}), f32[6,64,512]{2,1,0:T(8,128)}) %all-reduce.8.cloned.1.call-update) | async-done | bytes 786448 | tf_op jit(solution)/shard_map/psum | solution.py:12
  (438 shorter events, 230.6 us)
Async XLA Ops:
  10.8 9.2 slice-start
  12.2 7.9 slice-start.1
  22.9 6.8 slice-start.2
  55.8 92.8 %all-reduce.10.cloned.1.call-start = ((), (), s32[]{:S(2)}) async-start(), calls=%async_computation.2 | async-start | bytes 1572864 | tf_op jit(solution)/shard_map/while/body/eval_jaxpr/psum | solution.py:45
  68.2 4.6 copy-start.6
  68.2 4.6 copy-start.8
  70.6 112.3 %all-reduce.12.cloned.1.call-start = ((), (), s32[]{:S(2)}) async-start(), calls=%async_computation.3 | async-start | bytes 786432 | tf_op jit(solution)/shard_map/while/body/eval_jaxpr/psum | solution.py:12
  184.7 90.0 %all-reduce.10.cloned.1.call-start = ((), (), s32[]{:S(2)}) async-start(), calls=%async_computation.2 | async-start | bytes 1572864 | tf_op jit(solution)/shard_map/while/body/eval_jaxpr/psum | solution.py:45
  199.5 109.4 %all-reduce.12.cloned.1.call-start = ((), (), s32[]{:S(2)}) async-start(), calls=%async_computation.3 | async-start | bytes 786432 | tf_op jit(solution)/shard_map/while/body/eval_jaxpr/psum | solution.py:12
  310.7 90.0 %all-reduce.10.cloned.1.call-start = ((), (), s32[]{:S(2)}) async-start(), calls=%async_computation.2 | async-start | bytes 1572864 | tf_op jit(solution)/shard_map/while/body/eval_jaxpr/psum | solution.py:45
  325.5 109.4 %all-reduce.12.cloned.1.call-start = ((), (), s32[]{:S(2)}) async-start(), calls=%async_computation.3 | async-start | bytes 786432 | tf_op jit(solution)/shard_map/while/body/eval_jaxpr/psum | solution.py:12
  436.7 90.0 %all-reduce.10.cloned.1.call-start = ((), (), s32[]{:S(2)}) async-start(), calls=%async_computation.2 | async-start | bytes 1572864 | tf_op jit(solution)/shard_map/while/body/eval_jaxpr/psum | solution.py:45
  451.5 109.6 %all-reduce.12.cloned.1.call-start = ((), (), s32[]{:S(2)}) async-start(), calls=%async_computation.3 | async-start | bytes 786432 | tf_op jit(solution)/shard_map/while/body/eval_jaxpr/psum | solution.py:12
  562.9 90.0 %all-reduce.10.cloned.1.call-start = ((), (), s32[]{:S(2)}) async-start(), calls=%async_computation.2 | async-start | bytes 1572864 | tf_op jit(solution)/shard_map/while/body/eval_jaxpr/psum | solution.py:45
  577.6 109.4 %all-reduce.12.cloned.1.call-start = ((), (), s32[]{:S(2)}) async-start(), calls=%async_computation.3 | async-start | bytes 786432 | tf_op jit(solution)/shard_map/while/body/eval_jaxpr/psum | solution.py:12
  688.9 90.0 %all-reduce.10.cloned.1.call-start = ((), (), s32[]{:S(2)}) async-start(), calls=%async_computation.2 | async-start | bytes 1572864 | tf_op jit(solution)/shard_map/while/body/eval_jaxpr/psum | solution.py:45
  703.6 109.4 %all-reduce.12.cloned.1.call-start = ((), (), s32[]{:S(2)}) async-start(), calls=%async_computation.3 | async-start | bytes 786432 | tf_op jit(solution)/shard_map/while/body/eval_jaxpr/psum | solution.py:12
  814.9 90.0 %all-reduce.10.cloned.1.call-start = ((), (), s32[]{:S(2)}) async-start(), calls=%async_computation.2 | async-start | bytes 1572864 | tf_op jit(solution)/shard_map/while/body/eval_jaxpr/psum | solution.py:45
  829.6 109.4 %all-reduce.12.cloned.1.call-start = ((), (), s32[]{:S(2)}) async-start(), calls=%async_computation.3 | async-start | bytes 786432 | tf_op jit(solution)/shard_map/while/body/eval_jaxpr/psum | solution.py:12
  940.9 139.2 %all-reduce.6.cloned.1.call-start = ((), (), s32[]{:S(2)}) async-start(), calls=%async_computation | async-start | bytes 3145728 | tf_op jit(solution)/shard_map/psum | solution.py:50
  943.3 6.4 copy-start.17
  949.7 6.5 copy-start.14
  959.2 6.3 copy-start.15
  974.7 142.9 %all-reduce.8.cloned.1.call-start = ((), (), s32[]{:S(2)}) async-start(), calls=%async_computation.1 | async-start | bytes 1572864 | tf_op jit(solution)/shard_map/psum | solution.py:12
  (94 other events, 280.9 us)
Sparse Core Ops, SparseCore 0:
  70.7 77.7 all-reduce.9
  150.9 31.9 all-reduce.11
  199.6 75.0 all-reduce.9
  276.9 31.9 all-reduce.11
  325.6 75.0 all-reduce.9
  402.9 31.9 all-reduce.11
  451.6 75.0 all-reduce.9
  529.1 31.9 all-reduce.11
  577.7 75.0 all-reduce.9
  655.1 31.9 all-reduce.11
  703.7 75.0 all-reduce.9
  781.1 31.9 all-reduce.11
  829.7 75.0 all-reduce.9
  907.1 31.9 all-reduce.11
Sparse Core Ops, SparseCore 1:
  974.7 89.5 all-reduce.5
  1082.2 35.3 all-reduce.7
where the time goes:
time: 1140 us; the launch traced here: 1130 us
  waiting for transfers between devices  758 us (66%)
  local copies, waits for them, and re-layouts  149 us (13%)
  other arithmetic  87.8 us (8%)
  matrix products  57.9 us (5%)
  blocking collectives  40.9 us (4%)
  between operations  19 us (2%)
  loops' own time  14.8 us (1%)
    psum x7, waiting for transfers between devices, wave_units(): piece, root = own_block(lax.psum(partial_value, 'col'))  512 us
    psum x8, waiting for transfers between devices, from_root(): return lax.psum(block, axis)  245 us
    psum x1, blocking collectives, local(): lax.psum(partial_value, ('row', 'col'))  40.9 us
    another operation x23, other arithmetic  33.1 us
    dot_general x22, matrix products, contract_gates(): lax.dot_general(gate_flat, weight_flat, (((1,), (1,)), ((), ())), preferr...  32.2 us
    slice x7, local copies, waits for them, and re-layouts, diagonal_step(): gate_pre[layer]  24.9 us
  transfers between devices with their start and end apart: 16, of which 15 were waited for; matrix products, arithmetic and copies ran while one was open for 9% of the time, Pallas kernels for 0%

commit v1 on v0

v1 whole, which is shorter than its diff:
```python
import functools

import jax
import jax.numpy as jnp
from jax import lax
from jax.experimental import pallas as pl
from jax.experimental.pallas import tpu as pltpu
from jax.sharding import PartitionSpec as P

MESH = pl.DeviceIdType.MESH


def split_col(cols, ratio):
    fast = 1
    while fast * fast * 2 <= cols:
        fast *= 2
    while fast < ratio:
        fast *= 2
    return cols // fast, fast


def exchange_kernel(blocks, rows, cols, scalar, *refs):
    ratio = cols // rows
    slow_n, fast_n = split_col(cols, ratio)
    per = fast_n // ratio
    parts, refs = refs[:blocks], refs[blocks:]
    if scalar:
        sq_in, out, sq_out = refs[:3]
        refs = refs[3:]
    else:
        out = refs[0]
        refs = refs[1:]
    recv1, acc1, recv2, acc2, land, s1, r1, s2, r2, s3, r3 = refs[:11]
    if scalar:
        sq1, sqa1, sq2, sqa2, sq3, qs1, qr1, qs2, qr2, qs3, qr3 = refs[11:]
    width = recv1.shape[-1]
    mini = acc2.shape[1]
    row = lax.axis_index("row")
    col = lax.axis_index("col")
    slow, fast = col // fast_n, col % fast_n
    target = ratio * row + fast // per
    is_own = target == col
    source_row = col // ratio

    def fast_peer(d):
        return slow * fast_n + (fast + d) % fast_n

    def slow_peer(d):
        return ((slow + d) % slow_n) * fast_n + fast

    def source_col(z, j):
        return z * fast_n + (col % ratio) * per + j

    barrier = pltpu.get_barrier_semaphore()

    def greet(device):
        pl.semaphore_signal(barrier, inc=1, device_id=device, device_id_type=MESH)

    for d in range(1, fast_n):
        greet((row, fast_peer(d)))
    for d in range(1, slow_n):
        greet((row, slow_peer(d)))
    for z in range(slow_n):
        for j in range(per):
            other = source_col(z, j)

            @pl.when(jnp.logical_not((source_row == row) & (other == col)))
            def _(other=other):
                greet((source_row, other))

    count = fast_n - 1 + slow_n - 1 + rows - 1
    if scalar:
        for d in range(1, rows):
            greet(((row + d) % rows, col))
        count += rows - 1
    pl.semaphore_wait(barrier, count + jnp.where(is_own, 0, 1))

    def lanes(index):
        return pl.ds(pl.multiple_of(index * width, width), width)

    def subs(index):
        return pl.ds(pl.multiple_of(index * mini, mini), mini)

    def remote(src, dst, send, recv, device):
        return pltpu.make_async_remote_copy(
            src_ref=src, dst_ref=dst, send_sem=send, recv_sem=recv,
            device_id=device, device_id_type=MESH,
        )

    def copy1(b, d):
        peer = (fast + d) % fast_n
        return remote(parts[b].at[:, lanes(peer)], recv1.at[b, d - 1], s1.at[b, d - 1],
                      r1.at[b, d - 1], (row, fast_peer(d)))

    def copy2(b, d):
        peer = (slow + d) % slow_n
        return remote(acc1.at[b, subs(peer), :], recv2.at[b, d - 1], s2.at[b, d - 1],
                      r2.at[b, d - 1], (row, slow_peer(d)))

    def copy3(b, d):
        return remote(acc2.at[b], land.at[b, subs(slow), lanes(fast % per)], s3.at[b, d],
                      r3.at[b, slow * per + fast % per], ((row + d) % rows, target))

    def scalar1(d):
        return remote(sq_in, sq1.at[d - 1], qs1.at[d - 1], qr1.at[d - 1], (row, fast_peer(d)))

    def scalar2(d):
        return remote(sqa1, sq2.at[d - 1], qs2.at[d - 1], qr2.at[d - 1], (row, slow_peer(d)))

    def scalar3(d):
        return remote(sqa2, sq3.at[d - 1], qs3.at[d - 1], qr3.at[d - 1], ((row + d) % rows, col))

    if scalar:
        for d in range(1, fast_n):
            scalar1(d).start()
    for b in range(blocks):
        for d in range(1, fast_n):
            copy1(b, d).start()
    if scalar:
        value = sq_in[...]
        for d in range(1, fast_n):
            scalar1(d).wait_recv()
            value = value + sq1[d - 1]
        sqa1[...] = value
        for d in range(1, slow_n):
            scalar2(d).start()
    for b in range(blocks):
        value = parts[b][:, lanes(fast)]
        for d in range(1, fast_n):
            copy1(b, d).wait_recv()
            value = value + recv1[b, d - 1]
        acc1[b] = value
        for d in range(1, slow_n):
            copy2(b, d).start()
    if scalar:
        value = sqa1[...]
        for d in range(1, slow_n):
            scalar2(d).wait_recv()
            value = value + sq2[d - 1]
        sqa2[...] = value
        for d in range(1, rows):
            scalar3(d).start()
    for b in range(blocks):
        value = acc1[b, subs(slow), :]
        for d in range(1, slow_n):
            copy2(b, d).wait_recv()
            value = value + recv2[b, d - 1]
        acc2[b] = value

        @pl.when(is_own)
        def _(b=b, value=value):
            land[b, subs(slow), lanes(fast % per)] = value

        @pl.when(jnp.logical_not(is_own))
        def _(b=b):
            copy3(b, 0).start()

        for d in range(1, rows):
            copy3(b, d).start()
    if scalar:
        value = sqa2[...]
        for d in range(1, rows):
            scalar3(d).wait_recv()
            value = value + sq3[d - 1]
        sq_out[...] = value
    for b in range(blocks):
        for z in range(slow_n):
            for j in range(per):
                mine = (source_row == row) & (source_col(z, j) == col)

                @pl.when(jnp.logical_not(mine))
                def _(b=b, z=z, j=j):
                    spot = land.at[b, pl.ds(z * mini, mini), pl.ds(j * width, width)]
                    remote(spot, spot, s3.at[b, 0], r3.at[b, z * per + j],
                           (source_row, source_col(z, j))).wait_recv()

        out[b] = land[b]
    for b in range(blocks):
        for d in range(1, fast_n):
            copy1(b, d).wait_send()
        for d in range(1, slow_n):
            copy2(b, d).wait_send()
        for d in range(1, rows):
            copy3(b, d).wait_send()

        @pl.when(jnp.logical_not(is_own))
        def _(b=b):
            copy3(b, 0).wait_send()
    if scalar:
        for d in range(1, fast_n):
            scalar1(d).wait_send()
        for d in range(1, slow_n):
            scalar2(d).wait_send()
        for d in range(1, rows):
            scalar3(d).wait_send()


def exchange(parts, squares, collective):
    rows, cols = lax.axis_size("row"), lax.axis_size("col")
    ratio = cols // rows
    slow_n, fast_n = split_col(cols, ratio)
    blocks = len(parts)
    batch, units = parts[0].shape
    width, mini = units // fast_n, batch // slow_n
    scalar = squares is not None
    per = fast_n // ratio
    dma = pltpu.SemaphoreType.DMA
    vmem = lambda *shape: pltpu.VMEM(shape, jnp.float32)
    scratch = [
        vmem(blocks, fast_n - 1, batch, width), vmem(blocks, batch, width),
        vmem(blocks, slow_n - 1, mini, width), vmem(blocks, mini, width),
        vmem(blocks, batch, units // ratio),
        dma((blocks, fast_n - 1)), dma((blocks, fast_n - 1)),
        dma((blocks, slow_n - 1)), dma((blocks, slow_n - 1)),
        dma((blocks, rows)), dma((blocks, slow_n * per)),
    ]
    shapes = [jax.ShapeDtypeStruct((blocks, batch, units // ratio), jnp.float32)]
    args = list(parts)
    if scalar:
        args.append(squares)
        shapes.append(jax.ShapeDtypeStruct(squares.shape, jnp.float32))
        tile = squares.shape
        scratch += [
            vmem(fast_n - 1, *tile), vmem(*tile), vmem(slow_n - 1, *tile), vmem(*tile), vmem(rows - 1, *tile),
            dma((fast_n - 1,)), dma((fast_n - 1,)), dma((slow_n - 1,)), dma((slow_n - 1,)),
            dma((rows - 1,)), dma((rows - 1,)),
        ]
    in_vmem = pl.BlockSpec(memory_space=pltpu.VMEM)
    return pl.pallas_call(
        functools.partial(exchange_kernel, blocks, rows, cols, scalar),
        out_shape=shapes,
        in_specs=[in_vmem] * len(args),
        out_specs=[in_vmem] * len(shapes),
        scratch_shapes=scratch,
        compiler_params=pltpu.CompilerParams(collective_id=collective, has_side_effects=True),
        name="exchange",
    )(*args)


def cell_backward(preact, cell_prev, cell_now, hid_grad, cell_carry):
    in_gate = jax.nn.sigmoid(preact[:, 0])
    forget = jax.nn.sigmoid(preact[:, 1])
    cand_gate = jnp.tanh(preact[:, 2])
    out_gate = jax.nn.sigmoid(preact[:, 3])
    tanh_cell = jnp.tanh(cell_now)
    cell_grad = cell_carry + hid_grad * out_gate * (1.0 - tanh_cell * tanh_cell)
    grad_in = cell_grad * cand_gate * in_gate * (1.0 - in_gate)
    grad_forget = cell_grad * cell_prev * forget * (1.0 - forget)
    grad_cand = cell_grad * in_gate * (1.0 - cand_gate * cand_gate)
    grad_out = hid_grad * tanh_cell * out_gate * (1.0 - out_gate)
    gates = jnp.concatenate([grad_in, grad_forget, grad_cand, grad_out], axis=1)
    return (gates.astype(jnp.bfloat16), cell_grad * forget)


def contract(left, right, dims):
    return lax.dot_general(left, right, ((dims, dims), ((), ())), preferred_element_type=jnp.float32)


def local(w_rec, w_in, gate_pre, cells, layer_in, h_prev, top_grad):
    layers, row_units = w_rec.shape[:2]
    steps, batch, col_units = top_grad.shape
    rec_flats = [w_rec[layer].reshape(row_units, 4 * col_units) for layer in range(layers)]
    in_flats = [w_in[layer].reshape(row_units, 4 * col_units) for layer in range(layers)]
    zeros = jnp.zeros((batch, col_units), jnp.float32)
    recurrent = [zeros] * layers
    carry = [zeros] * layers
    incoming = [None] * layers
    store = [[None] * steps for _ in range(layers)]
    for diagonal in range(steps + layers - 1):
        parts, goes = [], []
        for layer in range(layers - 1, -1, -1):
            step = steps - 1 - diagonal + layers - 1 - layer
            if not 0 <= step < steps:
                continue
            outside = top_grad[step] if layer == layers - 1 else incoming[layer]
            gates, carry[layer] = cell_backward(
                gate_pre[layer, step], cells[layer, step], cells[layer, step + 1],
                outside + recurrent[layer], carry[layer],
            )
            store[layer][step] = gates
            if step > 0:
                parts.append(contract(gates, rec_flats[layer], (1,)))
                goes.append((recurrent, layer))
            if layer > 0:
                parts.append(contract(gates, in_flats[layer], (1,)))
                goes.append((incoming, layer - 1))
        if parts:
            units = exchange(parts, None, len(parts))[0]
            for index, (where, layer) in enumerate(goes):
                where[layer] = units[index]
    flats = [jnp.concatenate(store[layer], axis=0) for layer in range(layers)]
    rec_in = [h_prev[layer].reshape(steps * batch, row_units) for layer in range(layers)]
    lay_in = [layer_in[layer].reshape(steps * batch, row_units) for layer in range(layers)]
    sumsq = 0.0
    for layer in range(layers):
        inputs_gram = contract(rec_in[layer], rec_in[layer], (1,)) + contract(lay_in[layer], lay_in[layer], (1,))
        sumsq = sumsq + jnp.sum(inputs_gram * contract(flats[layer], flats[layer], (1,)))
    last = [contract(store[0][step], in_flats[0], (1,)) for step in range(steps)]
    input_grad, squares = exchange(last, jnp.broadcast_to(sumsq, (8, 128)), 0)
    entries = 2.0 * layers * (row_units * lax.axis_size("row")) * (4 * col_units * lax.axis_size("col"))
    scale = 1.0 / jnp.maximum(jnp.sqrt(squares[0, 0] / entries), 0.05)

    def weight_grad(inputs):
        return jnp.stack([
            (contract(inputs[layer], flats[layer], (0,)) * scale).astype(jnp.bfloat16)
            .reshape(row_units, 4, col_units)
            for layer in range(layers)
        ])

    return (weight_grad(rec_in), weight_grad(lay_in), input_grad)


def solution(mesh):
    placed = (
        P(None, "row", None, "col"),
        P(None, "row", None, "col"),
        P(None, None, None, None, "col"),
        P(None, None, None, "col"),
        P(None, None, None, "row"),
        P(None, None, None, "row"),
        P(None, None, "col"),
    )
    return jax.shard_map(
        local,
        mesh=mesh,
        in_specs=placed,
        out_specs=(P(None, "row", None, "col"), P(None, "row", None, "col"), P(None, None, "col")),
        check_vma=False,
    )
```

time: 1140 us -> 453 us (0.40)
  waiting for transfers between devices: 758 us -> 0 us
  Pallas kernels: 0 us -> 259 us
  local copies, waits for them, and re-layouts: 149 us -> 71.9 us
  other arithmetic: 87.8 us -> 37.6 us
  blocking collectives: 40.9 us -> 0 us
  loops' own time: 14.8 us -> 0 us
  matrix products: 57.9 us -> 72.4 us
  between operations: 19 us -> 4.91 us
    psum x16 -> x0, waiting for transfers between devices: 757 us -> none  [the longest x7 512 us: wave_units(): piece, root = own_block(lax.psum(partial_value, 'col'))]
    pallas_call x0 -> x7, Pallas kernels: none -> 259 us  [exchange(): pl.pallas_call(functools.partial(exchange_kernel, blocks, rows, cols, sca...]
    psum x1 -> x0, blocking collectives: 40.9 us -> none  [local(): lax.psum(partial_value, ('row', 'col'))]
    slice x14 -> x2, local copies, waits for them, and re-layouts: 36.7 us -> 6.78 us  [the longest x1 5.6 us: local(): gate_pre[layer, step]]
    select_n x29 -> x0, other arithmetic: 29.9 us -> none  [the longest x8 14.5 us: from_root(): jnp.where(lax.axis_index(axis) == owner, block, jnp.zeros_like(block))]
    another operation x39 -> x26, other arithmetic: 50.7 us -> 34.5 us  [the longest x2 17.5 us: weight_grad(): jnp.stack([(contract(inputs[layer], flats[layer], (0,)) * scale).astype(j...]
    another operation x20 -> x4, local copies, waits for them, and re-layouts: 47.3 us -> 31.5 us  [weight_grad(): jnp.stack([(contract(inputs[layer], flats[layer], (0,)) * scale).astype(j...]
    another operation x1 -> x0, loops' own time: 14.8 us -> none  [local(): lax.fori_loop(0, steps + layers - 1, diagonal_step, (zeros, zeros, zeros,...]
  transfers between devices with their start and end apart: 16 -> 0, of which waited for: 15 -> 0; matrix products, arithmetic and copies ran while one was open for 9% -> 0% of each run, Pallas kernels for 0% -> 0%
where the time goes in v1:
time: 453 us; the launch traced here: 445 us
  Pallas kernels  259 us (57%)
  matrix products  72.4 us (16%)
  local copies, waits for them, and re-layouts  71.9 us (16%)
  other arithmetic  37.6 us (8%)
  between operations  4.91 us (1%)
    pallas_call x7, Pallas kernels, exchange(): pl.pallas_call(functools.partial(exchange_kernel, blocks, rows, cols, sca...  259 us
    dot_general x32, matrix products, contract(): lax.dot_general(left, right, ((dims, dims), ((), ())), preferred_element_...  72.4 us
    another operation x4, local copies, waits for them, and re-layouts, weight_grad(): jnp.stack([(contract(inputs[layer], flats[layer], (0,)) * scale).astype(j...  31.5 us
    another operation x2, other arithmetic, weight_grad(): jnp.stack([(contract(inputs[layer], flats[layer], (0,)) * scale).astype(j...  17.5 us
    another operation x24, other arithmetic  17 us
    unnamed x295, local copies, waits for them, and re-layouts  13.4 us
    squeeze x6, local copies, waits for them, and re-layouts, local(): gate_pre[layer, step]  11 us

profile of v1, /device:TPU:0, one launch (start us, length us, event | category | flops | bytes accessed | tf_op | source)
XLA Modules:
  0.0 445.5 jit_solution(8062317137677841627)
XLA Ops:
  0.7 5.6 %fusion.294 = (f32[1,1,64,4,512]{4,3,2,1,0:T(4,128)}, f32[1,1,64,4,512]{4,3,2,1,0:T(4,128)}, f32[1,1,64,4,512]{4,3,2,1,0:T(4,128)}, f32[1,1,64,4,512]{4,3,2,1,0:...) fusion(f32[2,6,64,4,512]{4,3,2,1,0:T(4,128)} %param.9), kind=kLoop, calls=%fused_computation.458 | loop fusion | bytes 12582912 | tf_op jit(solution)/shard_map/slice | solution.py:277
  8.5 4.2 fusion.292
  16.3 4.1 fusion.293
  26.0 28.0 %exchange.7 = f32[2,64,512]{2,1,0:T(8,128)} custom-call(f32[64,1024]{1,0:T(8,128)} %fusion.279.refs_0_, f32[64,1024]{1,0:T(8,128)} %fusion.278.refs_1_), custom_call_target="tpu_custom_call" | custom-call | tf_op jit(solution)/shard_map/exchange/pallas_call | solution.py:229
  55.3 2.4 copy_bitcast_fusion.8
  68.5 36.3 %exchange.8 = f32[3,64,512]{2,1,0:T(8,128)} custom-call(f32[64,1024]{1,0:T(8,128)} %fusion.277.refs_0_, f32[64,1024]{1,0:T(8,128)} %fusion.276.refs_1_, f32[64,1024]{1,0:T(8,128)} %fusion.275.refs_2_), custom_call_target="tpu_custom_call" | custom-call | tf_op jit(solution)/shard_map/exchange/pallas_call | solution.py:229
  106.3 2.5 copy_bitcast_fusion.6
  116.5 33.6 %exchange.9 = f32[3,64,512]{2,1,0:T(8,128)} custom-call(f32[64,1024]{1,0:T(8,128)} %fusion.273.refs_0_, f32[64,1024]{1,0:T(8,128)} %fusion.272.refs_1_, f32[64,1024]{1,0:T(8,128)} %fusion.271.refs_2_), custom_call_target="tpu_custom_call" | custom-call | tf_op jit(solution)/shard_map/exchange/pallas_call | solution.py:229
  161.2 37.1 %exchange.10 = f32[3,64,512]{2,1,0:T(8,128)} custom-call(f32[64,1024]{1,0:T(8,128)} %fusion.269.refs_0_, f32[64,1024]{1,0:T(8,128)} %fusion.268.refs_1_, f32[64,1024]{1,0:T(8,128)} %fusion.267.refs_2_), custom_call_target="tpu_custom_call" | custom-call | tf_op jit(solution)/shard_map/exchange/pallas_call | solution.py:229
  209.3 33.7 %exchange.11 = f32[3,64,512]{2,1,0:T(8,128)} custom-call(f32[64,1024]{1,0:T(8,128)} %fusion.265.refs_0_, f32[64,1024]{1,0:T(8,128)} %fusion.264.refs_1_, f32[64,1024]{1,0:T(8,128)} %fusion.263.refs_2_), custom_call_target="tpu_custom_call" | custom-call | tf_op jit(solution)/shard_map/exchange/pallas_call | solution.py:229
  244.5 2.5 copy_bitcast_fusion
  253.3 26.3 %exchange.12 = f32[2,64,512]{2,1,0:T(8,128)} custom-call(f32[64,1024]{1,0:T(8,128)} %fusion.257.refs_0_, f32[64,1024]{1,0:T(8,128)} %fusion.261.refs_1_), custom_call_target="tpu_custom_call" | custom-call | tf_op jit(solution)/shard_map/exchange/pallas_call | solution.py:229
  292.8 3.6 copy.41
  309.3 63.7 %exchange.13 = (f32[6,64,512]{2,1,0:T(8,128)}, f32[8,128]{1,0:T(8,128)}) custom-call(f32[64,1024]{1,0:T(8,128)} %fusion.254.refs_0_, f32[64,1024]{1,0:T(8,128)} %fusion.260.refs_1_, f32[64,1024]{1,0:T(8,128)} %fusion.262.refs_2_, f32[64,1024]{1,0:T(8,128)} %fusion.266.refs_3_, f32[64,1024]{1,0:T(8,128)} %fusion.270.refs_4_, f32[64,1024]{1,0:T(8,128)} %fusion.274.refs_5_, ...), custom_call_target="tpu_custom_call" | custom-call | tf_op jit(solution)/shard_map/exchange/pallas_call | solution.py:229
  374.9 5.8 %multiply_convert_fusion.1 = bf16[2048,1024]{1,0:T(8,128)(2,1)} fusion(bf16[384,2048]{1,0:T(8,128)(2,1)} %copy-done.141, bf16[384,1024]{1,0:T(8,128)(2,1)S(1)} %bitcast.772, f32[]{:T(128)} %bitcast.90), kind=kOutput, calls=%fused_computation.3 | convolution fusion | flops 1614807040 | bytes 6553604 | tf_op jit(solution)/shard_map/dot_general | solution.py:256
  380.8 7.9 %copy.24 = bf16[1,1024,4,512]{3,2,1,0:T(4,128)(2,1)} copy(bf16[1,1024,4,512]{1,3,2,0:T(8,128)(2,1)} %bitcast.775) | data formatting | bytes 8388608 | tf_op jit(solution)/shard_map/stack;reshape | solution.py:304
  388.6 5.8 %multiply_convert_fusion = bf16[2048,1024]{1,0:T(8,128)(2,1)} fusion(bf16[384,2048]{1,0:T(8,128)(2,1)} %copy-done.139, bf16[384,1024]{1,0:T(8,128)(2,1)S(1)} %bitcast.770, f32[]{:T(128)} %bitcast.90), kind=kOutput, calls=%fused_computation.2 | convolution fusion | flops 1614807040 | bytes 6553604 | tf_op jit(solution)/shard_map/dot_general | solution.py:256
  394.4 7.8 %copy.25 = bf16[1,1024,4,512]{3,2,1,0:T(4,128)(2,1)} copy(bf16[1,1024,4,512]{1,3,2,0:T(8,128)(2,1)} %bitcast.776) | data formatting | bytes 8388608 | tf_op jit(solution)/shard_map/stack;reshape | solution.py:304
  402.3 8.8 %pad_maximum_fusion.1 = bf16[2,1024,4,512]{3,2,1,0:T(4,128)(2,1)} fusion(bf16[1,1024,4,512]{3,2,1,0:T(4,128)(2,1)} %copy.25, bf16[1,1024,4,512]{3,2,1,0:T(4,128)(2,1)} %copy.24), kind=kLoop, calls=%fused_computation.1 | loop fusion | flops 4194304 | bytes 16777216 | tf_op jit(solution)/shard_map/stack | solution.py:304
  411.0 4.4 multiply_convert_fusion.3
  415.5 8.0 %copy.22 = bf16[1,1024,4,512]{3,2,1,0:T(4,128)(2,1)} copy(bf16[1,1024,4,512]{1,3,2,0:T(8,128)(2,1)} %bitcast.774) | data formatting | bytes 8388608 | tf_op jit(solution)/shard_map/stack;reshape | solution.py:304
  423.4 4.4 multiply_convert_fusion.2
  427.8 7.9 %copy.23 = bf16[1,1024,4,512]{3,2,1,0:T(4,128)(2,1)} copy(bf16[1,1024,4,512]{1,3,2,0:T(8,128)(2,1)} %bitcast.773) | data formatting | bytes 8388608 | tf_op jit(solution)/shard_map/stack;reshape | solution.py:304
  435.7 8.7 %pad_maximum_fusion = bf16[2,1024,4,512]{3,2,1,0:T(4,128)(2,1)} fusion(bf16[1,1024,4,512]{3,2,1,0:T(4,128)(2,1)} %copy.23, bf16[1,1024,4,512]{3,2,1,0:T(4,128)(2,1)} %copy.22), kind=kLoop, calls=%fused_computation | loop fusion | flops 4194304 | bytes 16777216 | tf_op jit(solution)/shard_map/stack | solution.py:304
  (366 shorter events, 87.6 us)
Async XLA Ops:
  0.6 7.9 %copy-start.17 = (bf16[2,1024,4,512]{3,2,1,0:T(4,128)(2,1)S(1)}, bf16[2,1024,4,512]{3,2,1,0:T(4,128)(2,1)}, u32[]{:S(2)}) copy-start(bf16[2,1024,4,512]{3,2,1,0:T(4,128)(2,1)} %param.8) | copy-start | bytes 25165828
  8.4 13.5 %copy-start.66 = (bf16[64,512]{1,0:T(8,128)(2,1)}, bf16[64,512]{1,0:T(8,128)(2,1)S(1)}, u32[]{:S(2)}) copy-start(bf16[64,512]{1,0:T(8,128)(2,1)S(1)} %get-tuple-element.29) | copy-start | bytes 196612
  8.4 13.5 %copy-start.68 = (bf16[64,512]{1,0:T(8,128)(2,1)}, bf16[64,512]{1,0:T(8,128)(2,1)S(1)}, u32[]{:S(2)}) copy-start(bf16[64,512]{1,0:T(8,128)(2,1)S(1)} %get-tuple-element.52) | copy-start | bytes 196612
  8.4 8.0 %slice-start = ((s8[8388608]{0:T(1024)(128)(4,1)}), s8[4194304]{0:T(1024)(128)(4,1)S(1)}, s32[]{:S(2)}) async-start(s8[8388608]{0:T(1024)(128)(4,1)} %bitcast.763), calls=%async_computation | async-start | bytes 8388608
  8.5 13.4 %copy-start.76 = (bf16[64,512]{1,0:T(8,128)(2,1)}, bf16[64,512]{1,0:T(8,128)(2,1)S(1)}, u32[]{:S(2)}) copy-start(bf16[64,512]{1,0:T(8,128)(2,1)S(1)} %get-tuple-element.80) | copy-start | bytes 196612
  8.5 13.4 %copy-start.78 = (bf16[64,512]{1,0:T(8,128)(2,1)}, bf16[64,512]{1,0:T(8,128)(2,1)S(1)}, u32[]{:S(2)}) copy-start(bf16[64,512]{1,0:T(8,128)(2,1)S(1)} %get-tuple-element.81) | copy-start | bytes 196612
  64.2 40.6 %copy-start.19 = (f32[64,4,512]{2,0,1:T(8,128)S(1)}, f32[64,4,512]{2,0,1:T(8,128)}, u32[]{:S(2)}) copy-start(f32[64,4,512]{2,0,1:T(8,128)} %get-tuple-element.90) | copy-start | bytes 1572868
  112.3 37.9 %copy-start.21 = (f32[64,4,512]{2,0,1:T(8,128)S(1)}, f32[64,4,512]{2,0,1:T(8,128)}, u32[]{:S(2)}) copy-start(f32[64,4,512]{2,0,1:T(8,128)} %get-tuple-element.88) | copy-start | bytes 1572868
  112.3 37.9 %copy-start.26 = (f32[64,512]{1,0:T(8,128)S(1)}, f32[64,512]{1,0:T(8,128)}, u32[]{:S(2)}) copy-start(f32[64,512]{1,0:T(8,128)} %copy-done.25) | copy-start | bytes 393220
  153.2 46.5 %copy-start.20 = (f32[64,4,512]{2,0,1:T(8,128)}, f32[64,4,512]{2,0,1:T(8,128)S(1)}, u32[]{:S(2)}) copy-start(f32[64,4,512]{2,0,1:T(8,128)S(1)} %get-tuple-element.86) | copy-start | bytes 1572868
  157.0 41.3 %copy-start.28 = (f32[64,512]{1,0:T(8,128)S(1)}, f32[64,512]{1,0:T(8,128)}, u32[]{:S(2)}) copy-start(f32[64,512]{1,0:T(8,128)} %copy-done.27) | copy-start | bytes 393220
  205.0 38.0 %copy-start.24 = (f32[64,512]{1,0:T(8,128)S(1)}, f32[64,512]{1,0:T(8,128)}, u32[]{:S(2)}) copy-start(f32[64,512]{1,0:T(8,128)} %copy-done.23) | copy-start | bytes 393220
  250.4 29.3 %copy-start.22 = (f32[64,4,512]{2,0,1:T(8,128)S(1)}, f32[64,4,512]{2,0,1:T(8,128)}, u32[]{:S(2)}) copy-start(f32[64,4,512]{2,0,1:T(8,128)} %get-tuple-element.82) | copy-start | bytes 1572868
  251.1 30.0 %copy-start.60 = (bf16[64,512]{1,0:T(8,128)(2,1)S(1)}, bf16[64,512]{1,0:T(8,128)(2,1)}, u32[]{:S(2)}) copy-start(bf16[64,512]{1,0:T(8,128)(2,1)} %copy-done.59) | copy-start | bytes 196612
  251.1 31.0 %copy-start.53 = (bf16[64,512]{1,0:T(8,128)(2,1)S(1)}, bf16[64,512]{1,0:T(8,128)(2,1)}, u32[]{:S(2)}) copy-start(bf16[64,512]{1,0:T(8,128)(2,1)} %copy-done.52) | copy-start | bytes 196612
  251.1 32.0 %copy-start.46 = (bf16[64,512]{1,0:T(8,128)(2,1)S(1)}, bf16[64,512]{1,0:T(8,128)(2,1)}, u32[]{:S(2)}) copy-start(bf16[64,512]{1,0:T(8,128)(2,1)} %copy-done.45) | copy-start | bytes 196612
  251.1 32.9 %copy-start.43 = (bf16[64,512]{1,0:T(8,128)(2,1)S(1)}, bf16[64,512]{1,0:T(8,128)(2,1)}, u32[]{:S(2)}) copy-start(bf16[64,512]{1,0:T(8,128)(2,1)} %copy-done.42) | copy-start | bytes 196612
  251.2 33.0 %copy-start.36 = (bf16[64,512]{1,0:T(8,128)(2,1)S(1)}, bf16[64,512]{1,0:T(8,128)(2,1)}, u32[]{:S(2)}) copy-start(bf16[64,512]{1,0:T(8,128)(2,1)} %copy-done.35) | copy-start | bytes 196612
  251.2 33.0 %copy-start.71 = (bf16[64,512]{1,0:T(8,128)(2,1)S(1)}, bf16[64,512]{1,0:T(8,128)(2,1)}, u32[]{:S(2)}) copy-start(bf16[64,512]{1,0:T(8,128)(2,1)} %copy-done.70) | copy-start | bytes 196612
  251.2 33.0 %copy-start.74 = (bf16[64,512]{1,0:T(8,128)(2,1)S(1)}, bf16[64,512]{1,0:T(8,128)(2,1)}, u32[]{:S(2)}) copy-start(bf16[64,512]{1,0:T(8,128)(2,1)} %copy-done.73) | copy-start | bytes 196612
  251.2 33.0 %copy-start.81 = (bf16[64,512]{1,0:T(8,128)(2,1)S(1)}, bf16[64,512]{1,0:T(8,128)(2,1)}, u32[]{:S(2)}) copy-start(bf16[64,512]{1,0:T(8,128)(2,1)} %copy-done.80) | copy-start | bytes 196612
  402.3 8.8 %copy-start.142 = (bf16[384,2048]{1,0:T(8,128)(2,1)S(1)}, bf16[384,2048]{1,0:T(8,128)(2,1)}, u32[]{:S(2)}) copy-start(bf16[384,2048]{1,0:T(8,128)(2,1)} %copy-done.141) | copy-start | bytes 4718596
  415.5 8.0 %copy-start.140 = (bf16[384,2048]{1,0:T(8,128)(2,1)S(1)}, bf16[384,2048]{1,0:T(8,128)(2,1)}, u32[]{:S(2)}) copy-start(bf16[384,2048]{1,0:T(8,128)(2,1)} %copy-done.139) | copy-start | bytes 4718596
  435.7 8.7 %copy-start.126 = (f32[6,64,512]{2,1,0:T(8,128)S(1)}, f32[6,64,512]{2,1,0:T(8,128)}, u32[]{:S(2)}) copy-start(f32[6,64,512]{2,1,0:T(8,128)} %get-tuple-element.99) | copy-start | bytes 2359300
  (121 other events, 470.4 us)
